TPU v7x, 32 devices: a whole 2x2x4 slice. The times are simulated.
32 devices in a mesh: band: 16 (over z, y, x), chan: 2 (over core).
Axes of the slice: x: 2, y: 2, z: 4, core: 2. Of those that a mesh axis runs over, the one named last changes fastest.
Arguments:
- grid_latent: bfloat16 [18432, 512], P(('band', 'chan')), may hold values from -6 to 6
- edge_latent: bfloat16 [36864, 512], P(('band', 'chan')), may hold values from -6 to 6
- mesh_latent: bfloat16 [5120, 512], P(('band', 'chan')), may hold values from -6 to 6
- mesh_cotangent: bfloat16 [5120, 512], P(('band', 'chan')), may hold values from -6 to 6
- w_grid: bfloat16 [512, 512], P(None, 'chan'), may hold values from -0.15625 to 0.15625
- w_mesh: bfloat16 [512, 512], P(None, 'chan'), may hold values from -0.15625 to 0.15625
- w_edge: bfloat16 [512, 512], P(None, 'chan'), may hold values from -0.15625 to 0.15625
- bias: float32 [512], P('chan'), may hold values from -3 to 3
- w_out: bfloat16 [512, 512], P('chan'), may hold values from -0.25 to 0.25
- senders: int32 [36864], P('band'), may hold values from 0 to 18431, as said below
- receivers: int32 [36864], P('band'), may hold values from 0 to 5119, as said below
- edge_count: int32 [16], P('band'), may hold values from 1152 to 2304, as said below
Outputs:
- grad_grid: bfloat16 [18432, 512], P(('band', 'chan'))
- grad_edge: bfloat16 [36864, 512], P(('band', 'chan'))
- grad_mesh: bfloat16 [5120, 512], P(('band', 'chan'))
- grad_w_grid: float32 [512, 512], P(None, 'chan')
- grad_w_mesh: float32 [512, 512], P(None, 'chan')
- grad_w_edge: float32 [512, 512], P(None, 'chan')
- grad_bias: float32 [512], P('chan')
- grad_w_out: float32 [512, 512], P('chan')
Inputs may be any that keep to these rules, and one draw needn't show every extreme that they name: `senders`: an edge of band j (rows j * 2304 to (j + 1) * 2304 - 1) has its sender among grid rows j * 1152 to (j + 1) * 1152 - 1. `receivers`: an edge of band j has its receiver among mesh rows of owners j - 1, j, j + 1 (owner i holds rows i * 320 to (i + 1) * 320 - 1). `edge_count`: some band uses all 2304 slots.
All inputs are finite; a program needn't handle non-finite values.
Results may differ from a plain program's by a relative error of at most 0.0059.
Values may be sent and summed in bfloat16 or wider, within the bound.
A program may use at most 64 MiB of HBM per device.

v0:
```python
import jax
import jax.numpy as jnp
from jax import lax
from jax.sharding import PartitionSpec as P


def shifted(x, axis, by):
    devices = lax.axis_size(axis)
    pairs = [(i, i + by) for i in range(devices) if 0 <= i + by < devices]
    return lax.ppermute(x, axis, pairs)


def with_halo(x, sides, width):
    for axis, dim in sides:
        devices, length = (lax.axis_size(axis), x.shape[dim])
        up = [(i, (i + 1) % devices) for i in range(devices - 1)]
        down = [(j, i) for i, j in up]
        last = lax.slice_in_dim(x, length - width, length, axis=dim)
        initial = lax.slice_in_dim(x, 0, width, axis=dim)
        before = lax.ppermute(last, axis, up)
        after = lax.ppermute(initial, axis, down)
        x = jnp.concatenate([before, x, after], axis=dim)
    return x


def pass_rims(partial_value):
    from_lower = shifted(partial_value[2].astype(jnp.bfloat16), "band", 1).astype(jnp.float32)
    from_upper = shifted(partial_value[0], "band", -1)
    return partial_value[1] + from_lower + from_upper


def body(
    grid_latent,
    edge_latent,
    mesh_latent,
    mesh_cotangent,
    w_grid,
    w_mesh,
    w_edge,
    bias,
    w_out,
    senders,
    receivers,
    edge_count,
):
    band_index = lax.axis_index("band")
    grid_full = lax.all_gather(grid_latent, "chan", axis=0, tiled=True)
    edge_full = lax.all_gather(edge_latent, "chan", axis=0, tiled=True)
    stacked = lax.all_gather(jnp.stack([mesh_latent, mesh_cotangent]), "chan", axis=1, tiled=True)
    grid_rows = grid_full.shape[0]
    edge_rows = edge_full.shape[0]
    mesh_rows = stacked.shape[1]
    width = mesh_latent.shape[1]
    window = with_halo(stacked, (("band", 1),), mesh_rows)
    local_send = senders - band_index * grid_rows
    local_recv = receivers - (band_index - 1) * mesh_rows
    live = jnp.arange(edge_rows, dtype=jnp.int32) < edge_count[0]
    gsend = grid_full[local_send]
    mrecv = window[0][local_recv]
    message_cot = jnp.where(live[:, None], window[1][local_recv], jnp.zeros((), jnp.bfloat16))
    pre = (
        jnp.dot(gsend, w_grid, preferred_element_type=jnp.float32)
        + jnp.dot(mrecv, w_mesh, preferred_element_type=jnp.float32)
        + jnp.dot(edge_full, w_edge, preferred_element_type=jnp.float32)
        + bias
    )
    sig = jax.nn.sigmoid(pre)
    act = (pre * sig).astype(jnp.bfloat16)
    hidden_cot = lax.dot_general(
        message_cot, w_out, (((1,), (1,)), ((), ())), preferred_element_type=jnp.float32
    )
    pre_cot = (hidden_cot * sig * (1.0 + pre * (1.0 - sig))).astype(jnp.bfloat16)
    contract_rows = (((0,), (0,)), ((), ()))
    weight_terms = (
        lax.dot_general(gsend, pre_cot, contract_rows, preferred_element_type=jnp.float32),
        lax.dot_general(mrecv, pre_cot, contract_rows, preferred_element_type=jnp.float32),
        lax.dot_general(edge_full, pre_cot, contract_rows, preferred_element_type=jnp.float32),
        jnp.sum(pre_cot.astype(jnp.float32), axis=0),
        lax.dot_general(act, message_cot, contract_rows, preferred_element_type=jnp.float32),
    )
    grad_w_grid, grad_w_mesh, grad_w_edge, grad_bias, grad_w_out = lax.psum(
        (weight_terms[0], weight_terms[1], weight_terms[2], weight_terms[3], weight_terms[4]),
        "band",
    )
    contract_hidden = (((1,), (1,)), ((), ()))
    edge_terms = lax.dot_general(
        pre_cot, w_edge, contract_hidden, preferred_element_type=jnp.float32
    )
    grad_edge = lax.psum_scatter(
        edge_terms.astype(jnp.bfloat16), "chan", scatter_dimension=0, tiled=True
    )
    grid_terms = lax.dot_general(
        pre_cot, w_grid, contract_hidden, preferred_element_type=jnp.float32
    )
    grid_terms = jax.ops.segment_sum(grid_terms, local_send, num_segments=grid_rows)
    grad_grid = lax.psum_scatter(
        grid_terms.astype(jnp.bfloat16), "chan", scatter_dimension=0, tiled=True
    )
    mesh_terms = lax.dot_general(
        pre_cot, w_mesh, contract_hidden, preferred_element_type=jnp.float32
    )
    mesh_terms = jax.ops.segment_sum(mesh_terms, local_recv, num_segments=3 * mesh_rows)
    mesh_terms = mesh_terms.reshape(3, mesh_rows, width)
    reduced = lax.psum_scatter(mesh_terms, "chan", scatter_dimension=1, tiled=True)
    grad_mesh = pass_rims(reduced)
    return (
        grad_grid,
        grad_edge,
        grad_mesh.astype(jnp.bfloat16),
        grad_w_grid,
        grad_w_mesh,
        grad_w_edge,
        grad_bias,
        grad_w_out,
    )


def solution(mesh):
    return jax.shard_map(
        body,
        mesh=mesh,
        in_specs=(
            P(("band", "chan"), None),
            P(("band", "chan"), None),
            P(("band", "chan"), None),
            P(("band", "chan"), None),
            P(None, "chan"),
            P(None, "chan"),
            P(None, "chan"),
            P("chan"),
            P("chan", None),
            P("band"),
            P("band"),
            P("band"),
        ),
        out_specs=(
            P(("band", "chan"), None),
            P(("band", "chan"), None),
            P(("band", "chan"), None),
            P(None, "chan"),
            P(None, "chan"),
            P(None, "chan"),
            P("chan"),
            P("chan", None),
        ),
        check_vma=False,
    )
```

profile of v0, /device:TPU:0, one launch (start us, length us, event | category | flops | bytes accessed | tf_op | source)
XLA Modules:
  0.0 280.1 jit_solution(249288347982343971)
XLA Ops:
  7.2 0.0 copy-start
  7.2 0.0 all-gather.3.cloned.1.call-start
  7.2 0.7 all-gather.3.cloned.1.call-update
  7.9 0.0 all-gather.5.cloned.1.call-start
  8.0 0.7 all-gather.5.cloned.1.call-update
  8.7 0.0 reduce-scatter.8.cloned.1.call-start
  8.7 1.0 pad_maximum_fusion
  9.8 2.4 all_gather.9
  12.2 1.3 collective-permute-start.1
  13.4 5.4 %collective-permute-start = (bf16[2,320,512]{2,1,0:T(8,128)(2,1)S(1)}, bf16[2,320,512]{2,1,0:T(8,128)(2,1)S(1)}, u32[]{:S(2)}, u32[]{:S(2)}) collective-permute-start(bf16[2,320,512]{2,1,0:T(8,128)(2,1)S(1)} %all_gather.9), channel_id=1, source_target_pairs={{0,2},{2,4},{4,6},{6,8},{8,10},{10,12},{12,14},{14,16},{16,18},{18... | collective-permute-start | bytes 1966088 | tf_op jit(solution)/shard_map/ppermute | solution.py:20
  19.6 27.4 %collective-permute-done = bf16[2,320,512]{2,1,0:T(8,128)(2,1)S(1)} collective-permute-done((bf16[2,320,512]{2,1,0:T(8,128)(2,1)S(1)}, bf16[2,320,512]{2,1,0:T(8,128)(2,1)S(1)}, u32[]{:S(2)}, u32[]{:S(2)}) %collective-permute-start) | collective-permute-done | bytes 655392 | tf_op jit(solution)/shard_map/ppermute | solution.py:20
  47.2 0.0 collective-permute-done.1
  47.2 0.1 slice_bitcast_fusion.1
  47.4 7.5 %gather_fusion = bf16[2304,512]{1,0:T(8,128)(2,1)} fusion(bf16[960,512]{1,0:T(8,128)(2,1)S(1)} %get-tuple-element.32, s32[3072]{0:T(1024)S(1)} %pad_clamp_fusion.1), kind=kCustom, calls=%fused_computation | custom fusion | bytes 4727808 | tf_op jit(solution)/shard_map/gather | solution.py:60
  54.9 7.5 %gather_fusion.2 = bf16[2304,512]{1,0:T(8,128)(2,1)} fusion(bf16[960,512]{1,0:T(8,128)(2,1)S(1)} %get-tuple-element.33, s32[3072]{0:T(1024)S(1)} %pad_clamp_fusion.1), kind=kCustom, calls=%fused_computation.2 | custom fusion | bytes 4727808 | tf_op jit(solution)/shard_map/gather | solution.py:59
  62.4 8.5 %gather_fusion.1 = bf16[2304,512]{1,0:T(8,128)(2,1)S(1)} fusion(bf16[1152,512]{1,0:T(8,128)(2,1)} %all-gather.3.cloned.1.call-done, s32[3072]{0:T(1024)S(1)} %pad_clamp_fusion), kind=kCustom, calls=%fused_computation.1 | custom fusion | bytes 4727808 | tf_op jit(solution)/shard_map/gather | solution.py:58
  70.9 1.4 copy-done.3
  72.3 0.0 copy-done.10
  72.3 0.8 fusion.15
  73.1 0.0 copy-done
  73.1 0.9 copy-done.1
  74.0 0.8 convolution_add_fusion.1
  74.7 0.0 copy-start.17
  74.7 0.0 all-gather.5.cloned.1.call-done
  74.8 0.1 copy-done.9
  74.9 2.6 fusion
  77.5 2.3 convert_reduce_fusion
  79.8 0.0 copy-done.5
  79.8 3.0 %fusion.17 = f32[2304,512]{1,0:T(8,128)} fusion(bf16[2304,256]{1,0:T(8,128)(2,1)S(1)} %get-tuple-element.35, bf16[512,256]{1,0:T(8,128)(2,1)S(1)} %copy-done), kind=kOutput, calls=%fused_computation.47 | convolution fusion | flops 603979776 | bytes 6160384 | tf_op jit(solution)/shard_map/dot_general | solution.py:99
  82.8 17.6 %scatter_custom_fusion.1 = f32[960,512]{1,0:T(8,128)} fusion(s32[2304]{0:T(1024)S(1)} %get-tuple-element.29, f32[2304,512]{1,0:T(8,128)} %fusion.17, f32[]{:T(128)} %constant.10.clone.1), kind=kCustom, calls=%fused_computation.22 | custom fusion | flops 1179648 | bytes 1966592 | tf_op jit(solution)/shard_map/scatter-add | solution.py:102
  100.4 0.0 reduce-scatter.8.cloned.1.call-update
  100.5 0.2 all-reduce.3.cloned.1.call-start
  100.7 3.4 %convolution_bitcast_fusion = f32[512,256]{0,1:T(8,128)} fusion(bf16[2304,256]{1,0:T(8,128)(2,1)S(1)} %get-tuple-element.35, bf16[2304,512]{1,0:T(8,128)(2,1)} %all-gather.5.cloned.1.call-done), kind=kOutput, calls=%fused_computation.16 | convolution fusion | flops 603979776 | bytes 4063232 | tf_op jit(solution)/shard_map/dot_general | solution.py:77
  104.1 1.6 fusion.19
  105.7 0.1 copy-done.4
  105.8 1.6 fusion.18
  107.4 0.9 copy-done.6
  108.3 1.9 fusion.5
  110.2 0.0 all-reduce.3.cloned.1.call-update
  110.2 0.0 reduce-scatter.4.cloned.1.call-start
  110.3 2.9 %fusion.16 = f32[2304,512]{1,0:T(8,128)} fusion(bf16[2304,256]{1,0:T(8,128)(2,1)S(1)} %get-tuple-element.35, bf16[512,256]{1,0:T(8,128)(2,1)S(1)} %copy-done.10), kind=kOutput, calls=%fused_computation.46 | convolution fusion | flops 603979776 | bytes 6160384 | tf_op jit(solution)/shard_map/dot_general | solution.py:92
  113.2 17.8 %scatter_custom_fusion = f32[1152,512]{1,0:T(8,128)} fusion(s32[2304]{0:T(1024)S(1)} %get-tuple-element.31, f32[2304,512]{1,0:T(8,128)} %fusion.16, f32[]{:T(128)} %constant.10.clone.1), kind=kCustom, calls=%fused_computation.17 | custom fusion | flops 1179648 | bytes 2359808 | tf_op jit(solution)/shard_map/scatter-add | solution.py:95
  131.0 2.9 %convert_element_type.26 = bf16[1152,512]{1,0:T(8,128)(2,1)} convert(f32[1152,512]{1,0:T(8,128)} %scatter_custom_fusion) | non-fusion elementwise | flops 589824 | bytes 3538944 | tf_op jit(solution)/shard_map/convert_element_type | solution.py:97
  133.9 0.0 reduce-scatter.4.cloned.1.call-update
  133.9 0.0 reduce-scatter.6.cloned.1.call-start
  133.9 2.3 convolution_convert_fusion
  136.2 0.0 reduce-scatter.6.cloned.1.call-update
  136.2 0.0 reduce-scatter.8.cloned.1.call-done
  136.3 1.0 slice_bitcast_fusion.2
  137.3 1.3 collective-permute-start.3
  138.6 1.0 fusion.11
  139.6 5.0 %collective-permute-start.2 = (bf16[160,512]{1,0:T(8,128)(2,1)S(1)}, bf16[160,512]{1,0:T(8,128)(2,1)S(1)}, u32[]{:S(2)}, u32[]{:S(2)}) collective-permute-start(bf16[160,512]{1,0:T(8,128)(2,1)S(1)} %fusion.11), channel_id=1, source_target_pairs={{0,2},{2,4},{4,6},{6,8},{8,10},{10,12},{12,14},{14,16},{16,18},{18... | collective-permute-start | bytes 491528 | tf_op jit(solution)/shard_map/ppermute | solution.py:10
  144.6 42.9 %psum.38 = f32[256]{0:T(256)} all-reduce(f32[256]{0:T(256)S(1)} %get-tuple-element.34), channel_id=1, replica_groups=mesh['band'=16,'chan'=2] {'band'}, use_global_device_ids=true, to_apply=%region_9.10 | all-reduce | flops 256 | bytes 2048 | tf_op jit(solution)/shard_map/psum | solution.py:81
  187.5 58.8 %all-reduce.3.cloned.1.call-done = (f32[512,256]{1,0:T(8,128)}, f32[512,256]{1,0:T(8,128)}, f32[512,256]{0,1:T(8,128)}, f32[256,512]{1,0:T(8,128)}) async-done(((f32[512,256]{1,0:T(8,128)}, f32[512,256]{1,0:T(8,128)}, f32[512,256]{0,1:T(8,128)}, f32[256,512]{1,0:T(8,128)}), (f32[512,256]{1,0:T(8,128)}, f32[512,256]{1,0:T(8,128)}, f32[512,256]{0,1:T(8,128)}, ...) | async-done | bytes 2097168 | tf_op jit(solution)/shard_map/psum | solution.py:81
  246.4 2.2 copy.21
  248.5 0.0 collective-permute-done.2
  248.5 0.0 collective-permute-done.3
  248.5 1.7 fusion.10
  250.2 6.6 %reduce-scatter.4.cloned.1.call-done = bf16[576,512]{1,0:T(8,128)(2,1)} async-done(((bf16[1152,512]{1,0:T(8,128)(2,1)}), bf16[576,512]{1,0:T(8,128)(2,1)}) %reduce-scatter.4.cloned.1.call-update) | async-done | bytes 589840 | tf_op jit(solution)/shard_map/reduce_scatter | solution.py:96
  256.8 14.1 %reduce-scatter.6.cloned.1.call-done = bf16[1152,512]{1,0:T(8,128)(2,1)} async-done(((bf16[2304,512]{1,0:T(8,128)(2,1)}), bf16[1152,512]{1,0:T(8,128)(2,1)}) %reduce-scatter.6.cloned.1.call-update) | async-done | bytes 1179664 | tf_op jit(solution)/shard_map/reduce_scatter | solution.py:89
  270.9 0.8 copy.29
  271.7 0.0 copy-done.12
  271.7 0.8 copy.30
  272.5 0.8 copy.31
  (34 shorter events, 0.2 us)
Async XLA Ops:
  7.2 65.9 %copy-start = (bf16[512,256]{1,0:T(8,128)(2,1)S(1)}, bf16[512,256]{1,0:T(8,128)(2,1)}, u32[]{:S(2)}) copy-start(bf16[512,256]{1,0:T(8,128)(2,1)} %param.17) | copy-start | bytes 786436
  7.2 11.7 %copy-start.14 = (s32[2304]{0:T(1024)S(1)}, s32[2304]{0:T(1024)}, u32[]{:S(2)}) copy-start(s32[2304]{0:T(1024)} %param.21) | copy-start | bytes 27652
  7.2 12.4 %copy-start.15 = (s32[2304]{0:T(1024)S(1)}, s32[2304]{0:T(1024)}, u32[]{:S(2)}) copy-start(s32[2304]{0:T(1024)} %param.22) | copy-start | bytes 27652
  7.2 55.2 %all-gather.3.cloned.1.call-start = ((), (), s32[]{:S(2)}) async-start(), calls=%async_computation.3 | async-start | bytes 1769472 | tf_op jit(solution)/shard_map/all_gather | solution.py:47
  7.9 66.8 %all-gather.5.cloned.1.call-start = ((), (), s32[]{:S(2)}) async-start(), calls=%async_computation.4 | async-start | bytes 3538944 | tf_op jit(solution)/shard_map/all_gather | solution.py:48
  8.7 127.6 %reduce-scatter.8.cloned.1.call-start = ((), (), s32[]{:S(2)}) async-start(), calls=%async_computation.7 | async-start | bytes 2949120 | tf_op jit(solution)/shard_map/reduce_scatter | solution.py:104
  12.2 35.0 %collective-permute-start.1 = (bf16[2,320,512]{2,1,0:T(8,128)(2,1)S(1)}, bf16[2,320,512]{2,1,0:T(8,128)(2,1)S(1)}, u32[]{:S(2)}, u32[]{:S(2)}) collective-permute-start(bf16[2,320,512]{2,1,0:T(8,128)(2,1)S(1)} %all_gather.9), channel_id=1, source_target_pairs={{2,0},{4,2},{6,4},{8,6},{10,8},{12,10},{14,12},{16,14},{18,16},{20... | collective-permute-start | bytes 1966088 | tf_op jit(solution)/shard_map/ppermute | solution.py:21
  13.4 33.6 %collective-permute-start = (bf16[2,320,512]{2,1,0:T(8,128)(2,1)S(1)}, bf16[2,320,512]{2,1,0:T(8,128)(2,1)S(1)}, u32[]{:S(2)}, u32[]{:S(2)}) collective-permute-start(bf16[2,320,512]{2,1,0:T(8,128)(2,1)S(1)} %all_gather.9), channel_id=1, source_target_pairs={{0,2},{2,4},{4,6},{6,8},{8,10},{10,12},{12,14},{14,16},{16,18},{18... | collective-permute-start | bytes 1966088 | tf_op jit(solution)/shard_map/ppermute | solution.py:20
  62.4 9.9 %copy-start.10 = (bf16[512,256]{1,0:T(8,128)(2,1)S(1)}, bf16[512,256]{1,0:T(8,128)(2,1)}, u32[]{:S(2)}) copy-start(bf16[512,256]{1,0:T(8,128)(2,1)} %param.16) | copy-start | bytes 786436
  70.9 1.4 copy-start.3
  72.3 1.7 copy-start.1
  74.0 0.9 copy-start.9
  74.0 1.0 copy-start.16
  74.7 2.8 copy-start.17
  74.9 2.6 copy-start.7
  77.5 2.3 copy-start.5
  100.5 145.9 %all-reduce.3.cloned.1.call-start = ((), (), s32[]{:S(2)}) async-start(), calls=%async_computation.8 | async-start | bytes 4194304 | tf_op jit(solution)/shard_map/psum | solution.py:81
  100.7 3.4 %copy-start.2 = (bf16[2304,512]{1,0:T(8,128)(2,1)S(1)}, bf16[2304,512]{1,0:T(8,128)(2,1)}, u32[]{:S(2)}) copy-start(bf16[2304,512]{1,0:T(8,128)(2,1)} %gather_fusion.2) | copy-start | bytes 7077892
  104.1 1.7 copy-start.4
  104.1 3.3 %copy-start.8 = (bf16[2304,512]{1,0:T(8,128)(2,1)S(1)}, bf16[2304,512]{1,0:T(8,128)(2,1)}, u32[]{:S(2)}) copy-start(bf16[2304,512]{1,0:T(8,128)(2,1)} %gather_fusion) | copy-start | bytes 7077892
  105.8 2.5 copy-start.6
  110.2 146.5 %reduce-scatter.4.cloned.1.call-start = ((), (), s32[]{:S(2)}) async-start(), calls=%async_computation.5 | async-start | bytes 1769472 | tf_op jit(solution)/shard_map/reduce_scatter | solution.py:96
  133.9 137.0 %reduce-scatter.6.cloned.1.call-start = ((), (), s32[]{:S(2)}) async-start(), calls=%async_computation.6 | async-start | bytes 3538944 | tf_op jit(solution)/shard_map/reduce_scatter | solution.py:89
  137.3 111.3 %collective-permute-start.3 = (f32[160,512]{1,0:T(8,128)S(1)}, f32[160,512]{1,0:T(8,128)S(1)}, u32[]{:S(2)}, u32[]{:S(2)}) collective-permute-start(f32[160,512]{1,0:T(8,128)S(1)} %slice_bitcast_fusion.2), channel_id=1, source_target_pairs={{2,0},{4,2},{6,4},{8,6},{10,8},{12,10},{14,12},{16,14},{18,16},{20... | collective-permute-start | bytes 983048 | tf_op jit(solution)/shard_map/ppermute | solution.py:10
  139.6 109.0 %collective-permute-start.2 = (bf16[160,512]{1,0:T(8,128)(2,1)S(1)}, bf16[160,512]{1,0:T(8,128)(2,1)S(1)}, u32[]{:S(2)}, u32[]{:S(2)}) collective-permute-start(bf16[160,512]{1,0:T(8,128)(2,1)S(1)} %fusion.11), channel_id=1, source_target_pairs={{0,2},{2,4},{4,6},{6,8},{8,10},{10,12},{12,14},{14,16},{16,18},{18... | collective-permute-start | bytes 491528 | tf_op jit(solution)/shard_map/ppermute | solution.py:10
  246.4 24.5 %copy-start.13 = (f32[512,256]{1,0:T(8,128)S(1)}, f32[512,256]{1,0:T(8,128)}, u32[]{:S(2)}) copy-start(f32[512,256]{1,0:T(8,128)} %get-tuple-element.39) | copy-start | bytes 1572868
  246.4 25.3 %copy-start.12 = (f32[512,256]{1,0:T(8,128)S(1)}, f32[512,256]{1,0:T(8,128)}, u32[]{:S(2)}) copy-start(f32[512,256]{1,0:T(8,128)} %get-tuple-element.40) | copy-start | bytes 1572868
  246.4 26.1 %copy-start.11 = (f32[256,512]{1,0:T(8,128)S(1)}, f32[256,512]{1,0:T(8,128)}, u32[]{:S(2)}) copy-start(f32[256,512]{1,0:T(8,128)} %get-tuple-element.43) | copy-start | bytes 1572868
Sparse Core Ops, SparseCore 0:
  9.6 11.9 all-gather.2
  23.1 12.1 all-gather.4
  100.6 9.7 reduce-scatter.7
  116.8 129.5 all-reduce.2
  249.0 7.7 reduce-scatter.3
  259.5 11.3 reduce-scatter.5
where the time goes:
time: 281 us; the launch traced here: 280 us
  waiting for transfers between devices  108 us (38%)
  blocking collectives  45.3 us (16%)
  other arithmetic  41 us (15%)
  local copies, waits for them, and re-layouts  33.7 us (12%)
  matrix products  23.1 us (8%)
  between operations  15.1 us (5%)
  starting transfers between devices  13.4 us (5%)
    psum x1, waiting for transfers between devices, body(): lax.psum((weight_terms[0], weight_terms[1], weight_terms[2], weight_terms...  58.8 us
    psum x1, blocking collectives, body(): lax.psum((weight_terms[0], weight_terms[1], weight_terms[2], weight_terms...  42.9 us
    ppermute x1, waiting for transfers between devices, with_halo(): before = lax.ppermute(last, axis, up)  27.4 us
    scatter-add x1, other arithmetic, body(): jax.ops.segment_sum(grid_terms, local_send, num_segments=grid_rows)  17.8 us
    scatter-add x1, other arithmetic, body(): jax.ops.segment_sum(mesh_terms, local_recv, num_segments=3 * mesh_rows)  17.6 us
    reduce_scatter x1, waiting for transfers between devices, body(): lax.psum_scatter(edge_terms.astype(jnp.bfloat16), 'chan', scatter_dimensi...  14.1 us
    gather x1, local copies, waits for them, and re-layouts, body(): gsend = grid_full[local_send]  8.48 us
    unnamed x42, local copies, waits for them, and re-layouts  8.05 us
  transfers between devices with their start and end apart: 10, of which 4 were waited for; matrix products, arithmetic and copies ran while one was open for 24% of the time, Pallas kernels for 0%

commit v1 on v0

v1 whole, which is shorter than its diff:
```python
import functools

import jax
import jax.numpy as jnp
from jax import lax
from jax.experimental import pallas as pl
from jax.experimental.pallas import tpu as pltpu
from jax.sharding import PartitionSpec as P

BF = jnp.bfloat16
F32 = jnp.float32
MESH = pl.DeviceIdType.MESH
VMEM = pl.BlockSpec(memory_space=pltpu.VMEM)
ANY = pl.BlockSpec(memory_space=pl.ANY)
NN = (((1,), (0,)), ((), ()))
NT = (((1,), (1,)), ((), ()))
TN = (((0,), (0,)), ((), ()))


def mm(a, b, dims=NN):
    return lax.dot_general(a, b, dims, preferred_element_type=F32)


def remote(src, dst, send, recv, device):
    return pltpu.make_async_remote_copy(
        src_ref=src, dst_ref=dst, send_sem=send, recv_sem=recv,
        device_id=device, device_id_type=MESH,
    )


def gather_kernel(
    n, grid, edge, mesh, cot, w_mesh, w_out,
    grid_oth, edge_oth, mesh_oth, cot_oth, win, send, recv,
):
    me, half = lax.axis_index("band"), lax.axis_index("chan")
    up, down = lax.rem(me + 1, n), lax.rem(me + n - 1, n)
    partner = {"band": me, "chan": 1 - half}
    above, below = {"band": up, "chan": half}, {"band": down, "chan": half}
    barrier = pltpu.get_barrier_semaphore()
    for device in (partner, above, below):
        pl.semaphore_signal(barrier, inc=1, device_id=device, device_id_type=MESH)
    pl.semaphore_wait(barrier, 3)
    to_partner = [
        remote(src, dst, send.at[i], recv.at[i], partner)
        for i, (src, dst) in enumerate(
            ((mesh, mesh_oth), (cot, cot_oth), (grid, grid_oth), (edge, edge_oth))
        )
    ]
    for copy in to_partner:
        copy.start()
    rows, hidden = mesh.shape[0], w_mesh.shape[1]
    win[1, :rows, :hidden] = mm(mesh[...], w_mesh[...]).astype(BF)
    win[1, :rows, hidden:] = mm(cot[...], w_out[...], NT).astype(BF)
    to_partner[0].wait()
    to_partner[1].wait()
    win[1, rows:, :hidden] = mm(mesh_oth[...], w_mesh[...]).astype(BF)
    win[1, rows:, hidden:] = mm(cot_oth[...], w_out[...], NT).astype(BF)
    raise_up = remote(win.at[1], win.at[0], send.at[4], recv.at[4], above)
    lower = remote(win.at[1], win.at[2], send.at[5], recv.at[5], below)
    raise_up.start()
    lower.start()
    to_partner[2].wait()
    to_partner[3].wait()
    raise_up.wait()
    lower.wait()


def main_kernel(
    tiles, grid, grid_oth, edge, edge_oth, win, wg_t, we_t, bias, send, recv, live,
    grad_edge, grad_grid, rx, gwg, gwe, gbias,
    pg, pmc, sg, sr, ge, gb,
):
    t = pl.program_id(0)
    rows = grid.shape[0]
    hidden = wg_t.shape[0]
    window = win.shape[0]

    @pl.when(t == 0)
    def _():
        pg[:, :rows] = mm(wg_t[...], grid[...], NT).astype(BF)
        pg[:, rows:2 * rows] = mm(wg_t[...], grid_oth[...], NT).astype(BF)
        pad = pmc.shape[1] - window
        filled = win[...].astype(F32)
        if pad:
            filled = jnp.concatenate([filled, jnp.zeros((pad, 2 * hidden), F32)], axis=0)
        pmc[...] = filled.T.astype(BF)
        sg[...] = jnp.zeros_like(sg)
        sr[...] = jnp.zeros_like(sr)
        ge[...] = jnp.zeros_like(ge)
        gb[...] = jnp.zeros_like(gb)

    tile = edge.shape[0]
    x = jnp.where(t < tiles // 2, edge[...], edge_oth[...])
    s_t = jnp.where(
        lax.broadcasted_iota(jnp.int32, (2 * rows, tile), 0) == send[0], 1.0, 0.0
    ).astype(BF)
    r_t = jnp.where(
        lax.broadcasted_iota(jnp.int32, (pmc.shape[1], tile), 0) == recv[0], 1.0, 0.0
    ).astype(BF)
    both = mm(pmc[...], r_t)
    alive = live[0]
    pre = mm(pg[...], s_t) + both[:hidden] + mm(we_t[...], x, NT) + bias[...]
    sig = jax.nn.sigmoid(pre)
    act = (pre * sig * alive).astype(BF)
    pre_cot32 = both[hidden:] * alive * sig * (1.0 + pre * (1.0 - sig))
    pre_cot = pre_cot32.astype(BF)
    grad_edge[...] = mm(pre_cot, we_t[...], TN).astype(BF)
    sg[...] += mm(pre_cot, s_t, NT)
    sr[...] += mm(jnp.concatenate([pre_cot, act], axis=0), r_t, NT)
    ge[...] += mm(pre_cot, x)
    rounded = pre_cot.astype(F32)
    total = gb[...]
    for k in range(tile // 128):
        total = total + rounded[:, k * 128:(k + 1) * 128]
    gb[...] = total

    @pl.when(t == tiles - 1)
    def _():
        sums = sg[...].astype(BF)
        grad_grid[...] = mm(sums, wg_t[...], TN).astype(BF)
        gwg[...] = (
            mm(sums[:, :rows], grid[...]) + mm(sums[:, rows:], grid_oth[...])
        ).reshape(gwg.shape).astype(BF)
        gwe[...] = ge[...].reshape(gwe.shape).astype(BF)
        rx[...] = sr[...].T[:window].astype(BF)
        gbias[...] = jnp.broadcast_to(
            jnp.sum(gb[...].T, axis=0, keepdims=True), gbias.shape
        )


def reduce_kernel(
    n, grad_edge, grad_grid, rx, gwg, gwe, gbias, mesh, mesh_oth, cot, cot_oth, wm_t,
    edge_in, grid_in, mesh_in, mesh_own, out_a, out_b, bias_all,
    rims, mesh_send, own_b, in_a, in_b, chunk_a, chunk_b,
    send, recv, a_send, a_recv, b_send, b_recv, c_send, c_recv,
):
    me, half = lax.axis_index("band"), lax.axis_index("chan")
    up, down = lax.rem(me + 1, n), lax.rem(me + n - 1, n)
    partner = {"band": me, "chan": 1 - half}
    above, below = {"band": up, "chan": half}, {"band": down, "chan": half}

    def peer(k):
        return lax.rem(me + k, n)

    def device(k):
        return {"band": peer(k), "chan": half}

    def each(fn):
        def step(k, carry):
            fn(k)
            return carry
        lax.fori_loop(1, n, step, 0)

    barrier = pltpu.get_barrier_semaphore()
    pl.semaphore_signal(barrier, inc=1, device_id=partner, device_id_type=MESH)
    each(lambda k: pl.semaphore_signal(
        barrier, inc=1, device_id=device(k), device_id_type=MESH))
    pl.semaphore_wait(barrier, n)

    raise_up = remote(rx.at[2], rims.at[0], send.at[0], recv.at[0], above)
    lower = remote(rx.at[0], rims.at[1], send.at[1], recv.at[1], below)
    raise_up.start()
    lower.start()
    rows_e, rows_g = edge_in.shape[0], grid_in.shape[0]
    edge_copy = remote(
        grad_edge.at[pl.ds(rows_e, rows_e)], edge_in, send.at[2], recv.at[2], partner)
    grid_copy = remote(
        grad_grid.at[pl.ds(rows_g, rows_g)], grid_in, send.at[3], recv.at[3], partner)
    grid_copy.start()
    edge_copy.start()

    def a_copy(k, which, src):
        return remote(src.at[peer(k)], in_a.at[which, k], a_send.at[which, k],
                      a_recv.at[which, k], device(k))

    def bias_copy(k):
        return remote(gbias, bias_all.at[k], a_send.at[2, k], a_recv.at[2, k], device(k))

    def start_a(k):
        a_copy(k, 0, gwg).start()
        a_copy(k, 1, gwe).start()
        bias_copy(k).start()
    each(start_a)
    bias_all[0] = gbias[...]

    raise_up.wait()
    lower.wait()
    total = (rx[1].astype(F32) + rims[0].astype(F32) + rims[1].astype(F32)).astype(BF)
    hidden, rows = wm_t.shape[0], mesh.shape[0]
    mesh_part, act_part = total[:, :hidden], total[:, hidden:]
    part = mm(mesh_part, wm_t[...])
    mesh_send[...] = part[rows:].astype(BF)
    mesh_copy = remote(mesh_send, mesh_in, send.at[4], recv.at[4], partner)
    mesh_copy.start()
    mesh_own[...] = part[:rows].astype(BF)
    own_b[0] = (
        mm(mesh_part[:rows], mesh[...], TN) + mm(mesh_part[rows:], mesh_oth[...], TN)
    ).reshape(own_b.shape[1:]).astype(BF)
    own_b[1] = (
        mm(act_part[:rows], cot[...], TN) + mm(act_part[rows:], cot_oth[...], TN)
    ).reshape(own_b.shape[1:]).astype(BF)

    def b_copy(k, which):
        return remote(own_b.at[which, peer(k)], in_b.at[which, k], b_send.at[which, k],
                      b_recv.at[which, k], device(k))

    def start_b(k):
        b_copy(k, 0).start()
        b_copy(k, 1).start()
    each(start_b)

    def wait_a(k):
        a_copy(k, 0, gwg).wait()
        a_copy(k, 1, gwe).wait()
        bias_copy(k).wait()
    each(wait_a)
    in_a[0, 0] = gwg[me]
    in_a[1, 0] = gwe[me]
    chunk_a[...] = jnp.sum(in_a[...].astype(F32), axis=1).astype(BF)

    def gather_copy(k, which, chunk, out):
        return remote(chunk, out.at[me], c_send.at[which, k], c_recv.at[which, k], device(k))
    each(lambda k: gather_copy(k, 0, chunk_a, out_a).start())
    out_a[me] = chunk_a[...]

    def wait_b(k):
        b_copy(k, 0).wait()
        b_copy(k, 1).wait()
    each(wait_b)
    in_b[0, 0] = own_b[0, me]
    in_b[1, 0] = own_b[1, me]
    chunk_b[...] = jnp.sum(in_b[...].astype(F32), axis=1).astype(BF)
    each(lambda k: gather_copy(k, 1, chunk_b, out_b).start())
    out_b[me] = chunk_b[...]

    grid_copy.wait()
    edge_copy.wait()
    mesh_copy.wait()

    def finish(k):
        gather_copy(k, 0, chunk_a, out_a).wait()
        gather_copy(k, 1, chunk_b, out_b).wait()
    each(finish)


def body(
    grid_latent,
    edge_latent,
    mesh_latent,
    mesh_cotangent,
    w_grid,
    w_mesh,
    w_edge,
    bias,
    w_out,
    senders,
    receivers,
    edge_count,
):
    n = lax.axis_size("band")
    band, chan = lax.axis_index("band"), lax.axis_index("chan")
    rows_g, width = grid_latent.shape
    rows_e = edge_latent.shape[0]
    rows_m = mesh_latent.shape[0]
    hidden = w_grid.shape[1]
    own_m = 2 * rows_m
    sds = jax.ShapeDtypeStruct
    grid_oth, edge_oth, mesh_oth, cot_oth, win = pl.pallas_call(
        functools.partial(gather_kernel, n),
        out_shape=(
            sds(grid_latent.shape, BF), sds(edge_latent.shape, BF),
            sds(mesh_latent.shape, BF), sds(mesh_latent.shape, BF),
            sds((3, own_m, 2 * hidden), BF),
        ),
        in_specs=[ANY, ANY, VMEM, VMEM, VMEM, VMEM],
        out_specs=(ANY, ANY, VMEM, VMEM, VMEM),
        scratch_shapes=[pltpu.SemaphoreType.DMA((6,)), pltpu.SemaphoreType.DMA((6,))],
        compiler_params=pltpu.CompilerParams(collective_id=0, has_side_effects=True),
    )(grid_latent, edge_latent, mesh_latent, mesh_cotangent, w_mesh, w_out)

    tile = 384 if rows_e % 384 == 0 else rows_e
    tiles = 2 * rows_e // tile
    slot = jnp.arange(2 * rows_e, dtype=jnp.int32)
    own_first = lambda v: jnp.roll(v.reshape(2, rows_e), chan, axis=0).reshape(tiles, 1, tile)
    local_send = senders - (band * 2 + chan) * rows_g
    local_send = jnp.where(local_send < 0, local_send + 2 * rows_g, local_send)
    local_recv = receivers - (band - 1) * own_m
    owner, inner = local_recv // own_m, local_recv % own_m
    inner = inner - chan * rows_m
    local_recv = owner * own_m + jnp.where(inner < 0, inner + own_m, inner)
    live = (slot < edge_count[0]).astype(F32)
    pick = lambda v: own_first(v)
    wg_t, we_t, wm_t = w_grid.T, w_edge.T, w_mesh.T
    padded = -(-3 * own_m // 128) * 128
    chunk = hidden * width // (n * 256)
    whole = lambda shape: pl.BlockSpec(shape, lambda t: (0,) * len(shape))
    idx = pl.BlockSpec((1, 1, tile), lambda t: (t, 0, 0))
    mid = tiles // 2
    grad_edge, grad_grid, rx, gwg, gwe, gbias = pl.pallas_call(
        functools.partial(main_kernel, tiles),
        grid=(tiles,),
        out_shape=(
            sds((2 * rows_e, width), BF), sds((2 * rows_g, width), BF),
            sds((3 * own_m, 2 * hidden), BF),
            sds((hidden, width), BF), sds((hidden, width), BF),
            sds((8, hidden), F32),
        ),
        in_specs=[
            whole((rows_g, width)), whole((rows_g, width)),
            pl.BlockSpec((tile, width), lambda t: (jnp.minimum(t, mid - 1), 0)),
            pl.BlockSpec((tile, width), lambda t: (jnp.maximum(t - mid, 0), 0)),
            whole((3 * own_m, 2 * hidden)), whole((hidden, width)), whole((hidden, width)),
            whole((hidden, 1)), idx, idx, idx,
        ],
        out_specs=(
            pl.BlockSpec((tile, width), lambda t: (t, 0)),
            whole((2 * rows_g, width)), whole((3 * own_m, 2 * hidden)),
            whole((hidden, width)), whole((hidden, width)), whole((8, hidden)),
        ),
        scratch_shapes=[
            pltpu.VMEM((hidden, 2 * rows_g), BF), pltpu.VMEM((2 * hidden, padded), BF),
            pltpu.VMEM((hidden, 2 * rows_g), F32), pltpu.VMEM((2 * hidden, padded), F32),
            pltpu.VMEM((hidden, width), F32), pltpu.VMEM((hidden, 128), F32),
        ],
        compiler_params=pltpu.CompilerParams(dimension_semantics=("arbitrary",)),
    )(
        grid_latent, grid_oth, edge_latent, edge_oth,
        win.reshape(3 * own_m, 2 * hidden), wg_t, we_t, bias[:, None],
        pick(local_send), pick(local_recv), pick(live),
    )

    rows_c = hidden // n
    dma = pltpu.SemaphoreType.DMA
    chunked = (n, rows_c, width)
    edge_in, grid_in, mesh_in, mesh_own, out_a, out_b, bias_all = pl.pallas_call(
        functools.partial(reduce_kernel, n),
        out_shape=(
            sds((rows_e, width), BF), sds((rows_g, width), BF),
            sds((rows_m, width), BF), sds((rows_m, width), BF),
            sds((n, 2, rows_c, width), BF), sds((n, 2, rows_c, width), BF),
            sds((n, 8, hidden), F32),
        ),
        in_specs=[ANY, ANY] + [VMEM] * 9,
        out_specs=(ANY, ANY) + (VMEM,) * 5,
        scratch_shapes=[
            pltpu.VMEM((2, own_m, 2 * hidden), BF), pltpu.VMEM((rows_m, width), BF),
            pltpu.VMEM((2,) + chunked, BF), pltpu.VMEM((2,) + chunked, BF),
            pltpu.VMEM((2,) + chunked, BF), pltpu.VMEM((2, rows_c, width), BF),
            pltpu.VMEM((2, rows_c, width), BF),
            dma((5,)), dma((5,)), dma((3, n)), dma((3, n)), dma((2, n)), dma((2, n)),
            dma((2, n)), dma((2, n)),
        ],
        compiler_params=pltpu.CompilerParams(collective_id=1, has_side_effects=True),
    )(
        grad_edge, grad_grid, rx.reshape(3, own_m, 2 * hidden),
        gwg.reshape(chunked), gwe.reshape(chunked), gbias,
        mesh_latent, mesh_oth, mesh_cotangent, cot_oth, wm_t,
    )
    add = lambda a, b: (a.astype(F32) + b.astype(F32)).astype(BF)
    full = lambda out, i: out[:, i].reshape(hidden, width).astype(F32)
    return (
        add(grad_grid[:rows_g], grid_in),
        add(grad_edge[:rows_e], edge_in),
        add(mesh_own, mesh_in),
        full(out_a, 0).T,
        full(out_b, 0).T,
        full(out_a, 1).T,
        jnp.sum(bias_all[:, 0], axis=0),
        full(out_b, 1),
    )


def solution(mesh):
    rows = P(("band", "chan"), None)
    return jax.shard_map(
        body,
        mesh=mesh,
        in_specs=(
            rows, rows, rows, rows,
            P(None, "chan"), P(None, "chan"), P(None, "chan"), P("chan"), P("chan", None),
            P("band"), P("band"), P("band"),
        ),
        out_specs=(
            rows, rows, rows,
            P(None, "chan"), P(None, "chan"), P(None, "chan"), P("chan"), P("chan", None),
        ),
        check_vma=False,
    )
```

time: 281 us -> 130 us (0.46)
  Pallas kernels: 0 us -> 110 us
  waiting for transfers between devices: 108 us -> 0 us
  blocking collectives: 45.3 us -> 0 us
  other arithmetic: 41 us -> 9.43 us
  local copies, waits for them, and re-layouts: 33.7 us -> 8.31 us
  matrix products: 23.1 us -> 0 us
  between operations: 15.1 us -> 1.43 us
  starting transfers between devices: 13.4 us -> 0 us
    pallas_call x0 -> x3, Pallas kernels: none -> 110 us  [the longest x1 64.3 us: body(): pl.pallas_call(functools.partial(reduce_kernel, n), out_shape=(sds((rows_...]
    psum x1 -> x0, waiting for transfers between devices: 58.8 us -> none  [body(): lax.psum((weight_terms[0], weight_terms[1], weight_terms[2], weight_terms...]
    psum x1 -> x0, blocking collectives: 42.9 us -> none  [body(): lax.psum((weight_terms[0], weight_terms[1], weight_terms[2], weight_terms...]
    scatter-add x2 -> x0, other arithmetic: 35.4 us -> none  [the longest x1 17.8 us: body(): jax.ops.segment_sum(grid_terms, local_send, num_segments=grid_rows)]
    ppermute x4 -> x0, waiting for transfers between devices: 27.5 us -> none  [the longest x1 27.4 us: with_halo(): before = lax.ppermute(last, axis, up)]
    gather x3 -> x0, local copies, waits for them, and re-layouts: 23.5 us -> none  [the longest x1 8.48 us: body(): gsend = grid_full[local_send]]
    dot_general x11 -> x0, matrix products: 23.1 us -> none  [the longest x1 3.4 us: body(): lax.dot_general(edge_full, pre_cot, contract_rows, preferred_element_type...]
    reduce_scatter x3 -> x0, waiting for transfers between devices: 20.6 us -> none  [the longest x1 14.1 us: body(): lax.psum_scatter(edge_terms.astype(jnp.bfloat16), 'chan', scatter_dimensi...]
  transfers between devices with their start and end apart: 10 -> 0, of which waited for: 4 -> 0; matrix products, arithmetic and copies ran while one was open for 24% -> 0% of each run, Pallas kernels for 0% -> 0%
where the time goes in v1:
time: 130 us; the launch traced here: 129 us
  Pallas kernels  110 us (85%)
  other arithmetic  9.43 us (7%)
  local copies, waits for them, and re-layouts  8.31 us (6%)
  between operations  1.43 us (1%)
    pallas_call x1, Pallas kernels, body(): pl.pallas_call(functools.partial(reduce_kernel, n), out_shape=(sds((rows_...  64.3 us
    pallas_call x1, Pallas kernels, body(): pl.pallas_call(functools.partial(gather_kernel, n), out_shape=(sds(grid_l...  23.7 us
    pallas_call x1, Pallas kernels, body(): pl.pallas_call(functools.partial(main_kernel, tiles), grid=(tiles,), out_...  21.9 us
    convert_element_type x3, other arithmetic, body(): add = lambda a, b: (a.astype(F32) + b.astype(F32)).astype(BF)  5.33 us

profile of v1, /device:TPU:0, one launch (start us, length us, event | category | flops | bytes accessed | tf_op | source)
XLA Modules:
  0.0 129.1 jit_solution(7696617075859259518)
XLA Ops:
  0.7 0.7 compare_select_fusion.1
  1.4 0.7 fusion.2
  2.2 0.6 reshape.55.send
  2.8 0.6 reshape.57.recv
  4.1 0.6 reshape.58.live
  4.7 0.0 copy-start.6
  4.8 0.0 copy-start.7
  4.8 0.0 copy-start.8
  4.8 23.7 %shard_map.179 = (bf16[576,512]{1,0:T(8,128)(2,1)}, bf16[1152,512]{1,0:T(8,128)(2,1)}, bf16[160,512]{1,0:T(8,128)(2,1)}, bf16[160,512]{1,0:T(8,128)(2,1)}, bf16[3,320,512]{2,1,0:T(8,128)(2,1)}) custom-call(bf16[576,512]{1,0:T(8,128)(2,1)} %grid.3, bf16[1152,512]{1,0:T(8,128)(2,1)} %edge.3, bf16[160,512]{1,0:T(8,128)(2,1)} %mesh.3, bf16[160,512]{1,0:T(8,128)(2,1)} %cot.3, ...), custom_call_target="tpu_custom_call" | custom-call | tf_op jit(solution)/shard_map/pallas_call | solution.py:268
  28.5 0.0 copy-done.6
  28.5 0.8 copy.26
  29.4 0.0 copy-done.7
  29.4 0.8 copy.27
  30.2 0.0 copy-done.8
  30.2 0.8 copy.28.bias
  31.0 0.0 copy-start.2
  31.0 21.9 %shard_map.180 = (bf16[2304,512]{1,0:T(8,128)(2,1)}, bf16[1152,512]{1,0:T(8,128)(2,1)}, bf16[960,512]{1,0:T(8,128)(2,1)}, bf16[256,512]{1,0:T(8,128)(2,1)}, bf16[256,512]{1,0:T(8,128)(2,1)}, /*index=5*/f32[8,256]{1,0:T(8,128)}) custom-call(bf16[576,512]{1,0:T(8,128)(2,1)} %grid.3, bf16[576,512]{1,0:T(8,128)(2,1)} %get-tuple-element.27.grid_oth, ...), custom_call_target="tpu_custom_call" | custom-call | tf_op jit(solution)/shard_map/pallas_call | solution.py:299
  53.0 0.0 copy-done.2
  53.0 0.8 copy.29
  53.8 0.0 copy-start
  53.8 64.3 %shard_map.181 = (bf16[1152,512]{1,0:T(8,128)(2,1)}, bf16[576,512]{1,0:T(8,128)(2,1)}, bf16[160,512]{1,0:T(8,128)(2,1)}, bf16[160,512]{1,0:T(8,128)(2,1)}, bf16[...) custom-call(bf16[2304,512]{1,0:T(8,128)(2,1)} %get-tuple-element.31.grad_edge, ...), custom_call_target="tpu_custom_call" | custom-call | tf_op jit(solution)/shard_map/pallas_call | solution.py:335
  118.1 1.7 %add_convert_fusion.2 = bf16[160,512]{1,0:T(8,128)(2,1)} fusion(bf16[160,512]{1,0:T(8,128)(2,1)} %get-tuple-element.41, bf16[160,512]{1,0:T(8,128)(2,1)} %get-tuple-element.40), kind=kLoop, calls=%fused_computation.2 | loop fusion | flops 327680 | bytes 491520 | tf_op jit(solution)/shard_map/convert_element_type | solution.py:359
  119.8 0.0 copy-done
  119.8 0.0 copy-start.5
  119.8 2.7 %add_convert_fusion = bf16[1152,512]{1,0:T(8,128)(2,1)} fusion(bf16[1152,512]{1,0:T(8,128)(2,1)} %get-tuple-element.39, bf16[2304,512]{1,0:T(8,128)(2,1)S(1)} %copy-done), kind=kLoop, calls=%fused_computation | loop fusion | flops 2359296 | bytes 3538944 | tf_op jit(solution)/shard_map/convert_element_type | solution.py:359
  122.5 0.0 copy-done.5
  122.5 0.0 copy-start.4
  122.5 0.1 bitcast_convert_fusion.3
  122.6 1.0 copy.30
  123.6 0.0 copy-done.4
  123.6 0.1 bitcast_convert_fusion.2
  123.7 1.0 copy.31
  124.7 0.0 copy-start.1
  124.7 0.0 copy-start.3
  124.7 0.1 bitcast_convert_fusion.1
  124.8 1.0 copy.32
  125.8 0.9 bitcast_convert_fusion
  126.7 0.0 copy-done.1
  126.7 0.0 copy-done.3
  126.7 1.0 add_convert_fusion.1
  127.6 1.5 %slice_reduce_fusion = f32[256]{0:T(256)} fusion(f32[16,8,256]{2,1,0:T(8,128)} %get-tuple-element.44), kind=kLoop, calls=%fused_computation.17 | loop fusion | flops 3840 | bytes 17408 | tf_op jit(solution)/shard_map/reduce_sum | solution.py:368
  (7 shorter events, 0.2 us)
Async XLA Ops:
  4.7 23.8 %copy-start.6 = (bf16[512,256]{1,0:T(8,128)(2,1)S(1)}, bf16[512,256]{1,0:T(8,128)(2,1)}, u32[]{:S(2)}) copy-start(bf16[512,256]{1,0:T(8,128)(2,1)} %param.18) | copy-start | bytes 786436
  4.8 24.6 %copy-start.7 = (bf16[512,256]{1,0:T(8,128)(2,1)S(1)}, bf16[512,256]{1,0:T(8,128)(2,1)}, u32[]{:S(2)}) copy-start(bf16[512,256]{1,0:T(8,128)(2,1)} %param.20) | copy-start | bytes 786436
  4.8 25.4 %copy-start.8 = (f32[256]{0:T(256)S(1)}, f32[256]{0:T(256)}, u32[]{:S(2)}) copy-start(f32[256]{0:T(256)} %param.21) | copy-start | bytes 3076
  31.0 22.0 %copy-start.2 = (bf16[512,256]{1,0:T(8,128)(2,1)S(1)}, bf16[512,256]{1,0:T(8,128)(2,1)}, u32[]{:S(2)}) copy-start(bf16[512,256]{1,0:T(8,128)(2,1)} %w_mesh.1) | copy-start | bytes 786436
  53.8 66.0 %copy-start = (bf16[2304,512]{1,0:T(8,128)(2,1)S(1)}, bf16[2304,512]{1,0:T(8,128)(2,1)}, u32[]{:S(2)}) copy-start(bf16[2304,512]{1,0:T(8,128)(2,1)} %get-tuple-element.31.grad_edge) | copy-start | bytes 7077892
  119.8 2.7 %copy-start.5 = (bf16[16,2,16,512]{3,2,1,0:T(8,128)(2,1)S(1)}, bf16[16,2,16,512]{3,2,1,0:T(8,128)(2,1)}, u32[]{:S(2)}) copy-start(bf16[16,2,16,512]{3,2,1,0:T(8,128)(2,1)} %get-tuple-element.42) | copy-start | bytes 1572868
  122.5 1.1 copy-start.4
  124.7 2.0 %copy-start.1 = (bf16[1152,512]{1,0:T(8,128)(2,1)S(1)}, bf16[1152,512]{1,0:T(8,128)(2,1)}, u32[]{:S(2)}) copy-start(bf16[1152,512]{1,0:T(8,128)(2,1)} %get-tuple-element.30.grad_grid) | copy-start | bytes 3538948
  124.7 2.0 %copy-start.3 = (bf16[576,512]{1,0:T(8,128)(2,1)S(1)}, bf16[576,512]{1,0:T(8,128)(2,1)}, u32[]{:S(2)}) copy-start(bf16[576,512]{1,0:T(8,128)(2,1)} %get-tuple-element.38) | copy-start | bytes 1769476

commit v2 on v1

v2 whole, which is shorter than its diff:
```python
import functools

import jax
import jax.numpy as jnp
from jax import lax
from jax.experimental import pallas as pl
from jax.experimental.pallas import tpu as pltpu
from jax.sharding import PartitionSpec as P

BF = jnp.bfloat16
F32 = jnp.float32
MESH = pl.DeviceIdType.MESH
VMEM = pl.BlockSpec(memory_space=pltpu.VMEM)
ANY = pl.BlockSpec(memory_space=pl.ANY)
NN = (((1,), (0,)), ((), ()))
NT = (((1,), (1,)), ((), ()))
TN = (((0,), (0,)), ((), ()))


def mm(a, b, dims=NN):
    return lax.dot_general(a, b, dims, preferred_element_type=F32)


def remote(src, dst, send, recv, device):
    return pltpu.make_async_remote_copy(
        src_ref=src, dst_ref=dst, send_sem=send, recv_sem=recv,
        device_id=device, device_id_type=MESH,
    )


def gather_kernel(n, grid, edge, mesh, cot, grid_oth, edge_oth, win, send, recv, local):
    me, half = lax.axis_index("band"), lax.axis_index("chan")
    up, down = lax.rem(me + 1, n), lax.rem(me + n - 1, n)
    partner = {"band": me, "chan": 1 - half}
    above, below = {"band": up, "chan": half}, {"band": down, "chan": half}
    barrier = pltpu.get_barrier_semaphore()
    for device in (partner, above, below):
        pl.semaphore_signal(barrier, inc=1, device_id=device, device_id_type=MESH)
    pl.semaphore_wait(barrier, 3)
    copies = [
        remote(src, dst, send.at[i], recv.at[i], device)
        for i, (src, dst, device) in enumerate((
            (mesh, win.at[0, 0, 0], above), (cot, win.at[0, 0, 1], above),
            (mesh, win.at[2, 0, 0], below), (cot, win.at[2, 0, 1], below),
            (mesh, win.at[1, 1, 0], partner), (cot, win.at[1, 1, 1], partner),
            (grid, grid_oth, partner), (edge, edge_oth, partner),
        ))
    ]
    own = [
        pltpu.make_async_copy(src, win.at[1, 0, i], local.at[i])
        for i, src in enumerate((mesh, cot))
    ]
    for copy in copies + own:
        copy.start()
    forward = []
    for side in (0, 2):
        copies[side].wait()
        copies[side + 1].wait()
        i = 8 + side // 2
        forward.append(remote(
            win.at[side, 0], win.at[side, 1], send.at[i], recv.at[i], partner))
        forward[-1].start()
    for copy in own + copies[4:] + forward:
        copy.wait()


def turned(x):
    return x.astype(F32).T.astype(BF)


def main_kernel(
    tiles, own_m, scal, grid, grid_oth, edge, edge_oth, win, wg, we, wm, wo, bias, idx,
    grad_edge, grad_grid, rx, gall, gbias,
    wg_t, we_t, bcol, pg, pmc, sg, sr, ge, gb,
):
    t = pl.program_id(0)
    chan, band, count = scal[0], scal[1], scal[2]
    rows, width = grid.shape
    hidden = wg.shape[1]
    window = 3 * own_m
    pad = pmc.shape[1] - window

    def nodes(which):
        rows_in = win[:, :, which].reshape(window, width)
        if pad:
            rows_in = jnp.concatenate([rows_in, jnp.zeros((pad, width), BF)], axis=0)
        return rows_in

    @pl.when(t == 0)
    def _():
        wg_t[...] = turned(wg[...])
        we_t[...] = turned(we[...])
        bcol[...] = jnp.broadcast_to(bias[...], (128, hidden)).T
        pg[:, :rows] = mm(wg_t[...], grid[...], NT).astype(BF)
        pg[:, rows:2 * rows] = mm(wg_t[...], grid_oth[...], NT).astype(BF)
        pmc[:hidden] = mm(nodes(0), wm[...]).T.astype(BF)
        pmc[hidden:] = mm(wo[...], nodes(1), NT).astype(BF)
        sg[...] = jnp.zeros_like(sg)
        sr[...] = jnp.zeros_like(sr)
        ge[...] = jnp.zeros_like(ge)
        gb[...] = jnp.zeros_like(gb)

    tile = edge.shape[0]
    x = jnp.where(t < tiles // 2, edge[...], edge_oth[...])
    place = lax.rem(t + chan * (tiles // 2), tiles)
    from_row = idx[0, 0] - (2 * band + chan) * rows
    from_row = jnp.where(from_row < 0, from_row + 2 * rows, from_row)
    to_row = idx[1, 0] - (band - 1) * own_m
    owner = jnp.where(to_row >= 2 * own_m, 2 * own_m, jnp.where(to_row >= own_m, own_m, 0))
    inner = to_row - owner - chan * (own_m // 2)
    to_row = owner + jnp.where(inner < 0, inner + own_m, inner)
    slot = lax.broadcasted_iota(jnp.int32, (1, tile), 1) + place * tile
    alive = jnp.where(slot < count, 1.0, 0.0)
    s_t = jnp.where(
        lax.broadcasted_iota(jnp.int32, (2 * rows, tile), 0) == from_row, 1.0, 0.0
    ).astype(BF)
    r_t = jnp.where(
        lax.broadcasted_iota(jnp.int32, (pmc.shape[1], tile), 0) == to_row, 1.0, 0.0
    ).astype(BF)
    both = mm(pmc[...], r_t)
    pre = mm(pg[...], s_t) + both[:hidden] + mm(we_t[...], x, NT) + bcol[:, :1]
    sig = jax.nn.sigmoid(pre)
    act = (pre * sig * alive).astype(BF)
    pre_cot = (both[hidden:] * alive * sig * (1.0 + pre * (1.0 - sig))).astype(BF)
    grad_edge[...] = mm(pre_cot, we_t[...], TN).astype(BF)
    sg[...] += mm(pre_cot, s_t, NT)
    sr[...] += mm(jnp.concatenate([pre_cot, act], axis=0), r_t, NT)
    ge[...] += mm(pre_cot, x)
    rounded = pre_cot.astype(F32)
    total = gb[...]
    for k in range(tile // 128):
        total = total + rounded[:, k * 128:(k + 1) * 128]
    gb[...] = total

    @pl.when(t == tiles - 1)
    def _():
        sums = sg[...].astype(BF)
        grad_grid[...] = mm(sums, wg_t[...], TN).astype(BF)
        parts = gall.shape[1:2] + gall.shape[3:]
        put = lambda v: v.reshape(parts).astype(BF)
        gall[0, :, 0] = put(mm(sums[:, :rows], grid[...]) + mm(sums[:, rows:], grid_oth[...]))
        gall[0, :, 1] = put(ge[...])
        mesh_sums = sr[:hidden]
        gall[1, :, 0] = put(mm(mesh_sums.astype(BF), nodes(0)))
        gall[1, :, 1] = put(mm(sr[hidden:].astype(BF), nodes(1)))
        rx[...] = mesh_sums.T[:window].astype(BF)
        gbias[...] = jnp.broadcast_to(
            jnp.sum(gb[...].T, axis=0, keepdims=True), gbias.shape
        )


def reduce_kernel(
    low, high, grad_edge, grad_grid, rx, gall, gbias, wm,
    edge_in, grid_in, mesh_in, mesh_own, out, bias_out,
    rims, mesh_send, in1, sum1, in2, sum2, out1, bias_in, bias_sum,
    send, recv, s1, r1, s2, r2, s3, r3, s4, r4, sb, rb, sc, rc,
):
    n = low * high
    me, half = lax.axis_index("band"), lax.axis_index("chan")
    mine, plane = lax.rem(me, low), me // low
    up, down = lax.rem(me + 1, n), lax.rem(me + n - 1, n)
    partner = {"band": me, "chan": 1 - half}
    above, below = {"band": up, "chan": half}, {"band": down, "chan": half}

    def low_peer(k):
        return lax.rem(mine + k, low)

    def low_device(k):
        return {"band": plane * low + low_peer(k), "chan": half}

    def high_peer(k):
        return lax.rem(plane + k, high)

    def high_device(k):
        return {"band": high_peer(k) * low + mine, "chan": half}

    barrier = pltpu.get_barrier_semaphore()

    def greet(k, carry):
        pl.semaphore_signal(
            barrier, inc=1, device_id={"band": lax.rem(me + k, n), "chan": half},
            device_id_type=MESH)
        return carry
    pl.semaphore_signal(barrier, inc=1, device_id=partner, device_id_type=MESH)
    lax.fori_loop(1, n, greet, 0)
    pl.semaphore_wait(barrier, n)

    def scatter_low(k, ab):
        return remote(gall.at[ab, low_peer(k)], in1.at[ab, k], s1.at[ab, k], r1.at[ab, k],
                      low_device(k))

    def scatter_high(k, ab):
        return remote(sum1.at[ab, high_peer(k)], in2.at[ab, k], s2.at[ab, k], r2.at[ab, k],
                      high_device(k))

    def gather_high(k, ab):
        return remote(sum2.at[ab], out1.at[ab, plane], s3.at[ab, k], r3.at[ab, k],
                      high_device(k))

    def gather_low(k, ab):
        return remote(out1.at[ab], out.at[ab, mine], s4.at[ab, k], r4.at[ab, k],
                      low_device(k))

    def bias_low(k):
        return remote(gbias, bias_in.at[mine], sb.at[k], rb.at[k], low_device(k))

    def bias_high(k):
        return remote(bias_sum, bias_out.at[plane], sc.at[k], rc.at[k], high_device(k))

    lows, highs = range(1, low), range(1, high)
    for k in lows:
        scatter_low(k, 0).start()
    for k in lows:
        bias_low(k).start()
    raise_up = remote(rx.at[2], rims.at[0], send.at[0], recv.at[0], above)
    lower = remote(rx.at[0], rims.at[1], send.at[1], recv.at[1], below)
    rows_e, rows_g, rows_m = edge_in.shape[0], grid_in.shape[0], mesh_own.shape[0]
    edge_copy = remote(
        grad_edge.at[pl.ds(rows_e, rows_e)], edge_in, send.at[2], recv.at[2], partner)
    grid_copy = remote(
        grad_grid.at[pl.ds(rows_g, rows_g)], grid_in, send.at[3], recv.at[3], partner)
    for k in lows:
        scatter_low(k, 1).start()
    grid_copy.start()
    edge_copy.start()
    raise_up.start()
    lower.start()
    bias_in[mine] = gbias[...]

    def reduce_low(ab):
        for k in lows:
            scatter_low(k, ab).wait()
        total = gall[ab, mine].astype(F32)
        for k in lows:
            total = total + in1[ab, k].astype(F32)
        sum1[ab] = total.astype(BF)
        for k in highs:
            scatter_high(k, ab).start()

    def reduce_high(ab):
        for k in highs:
            scatter_high(k, ab).wait()
        total = sum1[ab, plane].astype(F32)
        for k in highs:
            total = total + in2[ab, k].astype(F32)
        sum2[ab] = total.astype(BF)
        for k in highs:
            gather_high(k, ab).start()
        out1[ab, plane] = sum2[ab]

    def spread(ab):
        for k in highs:
            gather_high(k, ab).wait()
        for k in lows:
            gather_low(k, ab).start()
        out[ab, mine] = out1[ab]

    reduce_low(0)
    for k in lows:
        bias_low(k).wait()
    bias_sum[...] = jnp.sum(bias_in[...], axis=0)
    for k in highs:
        bias_high(k).start()
    bias_out[plane] = bias_sum[...]
    reduce_high(0)
    reduce_low(1)
    spread(0)
    reduce_high(1)
    raise_up.wait()
    lower.wait()
    total = (rx[1].astype(F32) + rims[0].astype(F32) + rims[1].astype(F32)).astype(BF)
    part = mm(total, wm[...], NT)
    mesh_send[...] = part[rows_m:].astype(BF)
    mesh_copy = remote(mesh_send, mesh_in, send.at[4], recv.at[4], partner)
    mesh_copy.start()
    mesh_own[...] = part[:rows_m].astype(BF)
    spread(1)
    grid_copy.wait()
    edge_copy.wait()
    mesh_copy.wait()
    for k in highs:
        bias_high(k).wait()
    for ab in (0, 1):
        for k in lows:
            gather_low(k, ab).wait()


def final_kernel(
    grid_own, grid_in, edge_own, edge_in, mesh_own, mesh_in, out, bias_out,
    grad_grid, grad_edge, grad_mesh, gwg, gwm, gwe, gbias, gwo,
):
    for a, b, to in (
        (grid_own, grid_in, grad_grid), (edge_own, edge_in, grad_edge),
        (mesh_own, mesh_in, grad_mesh),
    ):
        to[...] = (a[...].astype(F32) + b[...].astype(F32)).astype(BF)
    full = lambda ab, i: out[ab, :, i].astype(F32).reshape(gwo.shape)
    gwg[...] = full(0, 0).T
    gwe[...] = full(0, 1).T
    gwm[...] = full(1, 0).T
    gwo[...] = full(1, 1)
    gbias[...] = jnp.sum(bias_out[...], axis=0)


def body(
    grid_latent,
    edge_latent,
    mesh_latent,
    mesh_cotangent,
    w_grid,
    w_mesh,
    w_edge,
    bias,
    w_out,
    senders,
    receivers,
    edge_count,
):
    n = lax.axis_size("band")
    band, chan = lax.axis_index("band"), lax.axis_index("chan")
    rows_g, width = grid_latent.shape
    rows_e = edge_latent.shape[0]
    rows_m = mesh_latent.shape[0]
    hidden = w_grid.shape[1]
    own_m = 2 * rows_m
    sds = jax.ShapeDtypeStruct
    dma = pltpu.SemaphoreType.DMA
    grid_oth, edge_oth, win = pl.pallas_call(
        functools.partial(gather_kernel, n),
        out_shape=(
            sds(grid_latent.shape, BF), sds(edge_latent.shape, BF),
            sds((3, 2, 2, rows_m, width), BF),
        ),
        in_specs=[ANY, ANY, VMEM, VMEM],
        out_specs=(ANY, ANY, VMEM),
        scratch_shapes=[dma((10,)), dma((10,)), dma((2,))],
        compiler_params=pltpu.CompilerParams(collective_id=0, has_side_effects=True),
    )(grid_latent, edge_latent, mesh_latent, mesh_cotangent)

    tile = 384 if rows_e % 384 == 0 else rows_e
    tiles = 2 * rows_e // tile
    mid = tiles // 2
    padded = -(-3 * own_m // 128) * 128
    low = 1
    while low * low < n:
        low *= 2
    high = n // low
    rows_c = hidden // n
    scal = jnp.stack([chan, band, edge_count[0]]).astype(jnp.int32)
    idx = jnp.stack([senders, receivers]).reshape(2, tiles, 1, tile)
    whole = lambda *shape: pl.BlockSpec(shape, lambda t, s: (0,) * len(shape))
    grad_edge, grad_grid, rx, gall, gbias = pl.pallas_call(
        functools.partial(main_kernel, tiles, own_m),
        grid_spec=pltpu.PrefetchScalarGridSpec(
            num_scalar_prefetch=1,
            grid=(tiles,),
            in_specs=[
                whole(rows_g, width), whole(rows_g, width),
                pl.BlockSpec((tile, width), lambda t, s: (jnp.minimum(t, mid - 1), 0)),
                pl.BlockSpec((tile, width), lambda t, s: (jnp.maximum(t - mid, 0), 0)),
                whole(3, 2, 2, rows_m, width),
                whole(width, hidden), whole(width, hidden), whole(width, hidden),
                whole(hidden, width), whole(1, hidden),
                pl.BlockSpec(
                    (2, 1, 1, tile), lambda t, s: (0, lax.rem(t + s[0] * mid, tiles), 0, 0)),
            ],
            out_specs=(
                pl.BlockSpec((tile, width), lambda t, s: (t, 0)),
                whole(2 * rows_g, width), whole(3 * own_m, hidden),
                whole(2, n, 2, rows_c, width), whole(8, hidden),
            ),
            scratch_shapes=[
                pltpu.VMEM((hidden, width), BF), pltpu.VMEM((hidden, width), BF),
                pltpu.VMEM((hidden, 128), F32),
                pltpu.VMEM((hidden, 2 * rows_g), BF), pltpu.VMEM((2 * hidden, padded), BF),
                pltpu.VMEM((hidden, 2 * rows_g), F32), pltpu.VMEM((2 * hidden, padded), F32),
                pltpu.VMEM((hidden, width), F32), pltpu.VMEM((hidden, 128), F32),
            ],
        ),
        out_shape=(
            sds((2 * rows_e, width), BF), sds((2 * rows_g, width), BF),
            sds((3 * own_m, hidden), BF),
            sds((2, n, 2, rows_c, width), BF), sds((8, hidden), F32),
        ),
        compiler_params=pltpu.CompilerParams(dimension_semantics=("arbitrary",)),
    )(
        scal, grid_latent, grid_oth, edge_latent, edge_oth, win,
        w_grid, w_edge, w_mesh, w_out, bias[None], idx,
    )

    blocks = (2, rows_c, width)
    edge_in, grid_in, mesh_in, mesh_own, out, bias_out = pl.pallas_call(
        functools.partial(reduce_kernel, low, high),
        out_shape=(
            sds((rows_e, width), BF), sds((rows_g, width), BF),
            sds((rows_m, width), BF), sds((rows_m, width), BF),
            sds((2, low, high) + blocks, BF), sds((high, 8, hidden), F32),
        ),
        in_specs=[ANY, ANY] + [VMEM] * 4,
        out_specs=(ANY, ANY) + (VMEM,) * 4,
        scratch_shapes=[
            pltpu.VMEM((2, own_m, hidden), BF), pltpu.VMEM((rows_m, width), BF),
            pltpu.VMEM((2, low, high) + blocks, BF), pltpu.VMEM((2, high) + blocks, BF),
            pltpu.VMEM((2, high) + blocks, BF), pltpu.VMEM((2,) + blocks, BF),
            pltpu.VMEM((2, high) + blocks, BF),
            pltpu.VMEM((low, 8, hidden), F32), pltpu.VMEM((8, hidden), F32),
            dma((5,)), dma((5,)), dma((2, low)), dma((2, low)), dma((2, high)),
            dma((2, high)), dma((2, high)), dma((2, high)), dma((2, low)), dma((2, low)),
            dma((low,)), dma((low,)), dma((high,)), dma((high,)),
        ],
        compiler_params=pltpu.CompilerParams(collective_id=1, has_side_effects=True),
    )(
        grad_edge, grad_grid, rx.reshape(3, own_m, hidden),
        gall.reshape((2, low, high) + blocks), gbias, w_mesh,
    )

    rows_of = lambda rows: pl.BlockSpec((rows // 2, width), lambda t: (t, 0))
    turned_spec = pl.BlockSpec((width, hidden // 2), lambda t: (0, t))
    grad_grid, grad_edge, grad_mesh, gwg, gwm, gwe, gbias, gwo = pl.pallas_call(
        final_kernel,
        grid=(2,),
        in_specs=[
            rows_of(rows_g), rows_of(rows_g), rows_of(rows_e), rows_of(rows_e),
            rows_of(rows_m), rows_of(rows_m),
            pl.BlockSpec((2, n // 2) + blocks, lambda t: (0, t, 0, 0, 0)),
            pl.BlockSpec((high, 8, hidden), lambda t: (0, 0, 0)),
        ],
        out_specs=(
            rows_of(rows_g), rows_of(rows_e), rows_of(rows_m),
            turned_spec, turned_spec, turned_spec,
            pl.BlockSpec((8, hidden), lambda t: (0, 0)), rows_of(hidden),
        ),
        out_shape=(
            sds((rows_g, width), BF), sds((rows_e, width), BF), sds((rows_m, width), BF),
            sds((width, hidden), F32), sds((width, hidden), F32), sds((width, hidden), F32),
            sds((8, hidden), F32), sds((hidden, width), F32),
        ),
        compiler_params=pltpu.CompilerParams(dimension_semantics=("arbitrary",)),
    )(
        grad_grid, grid_in, grad_edge, edge_in, mesh_own, mesh_in,
        out.reshape((2, n) + blocks), bias_out,
    )
    return grad_grid, grad_edge, grad_mesh, gwg, gwm, gwe, gbias[0], gwo


def solution(mesh):
    rows = P(("band", "chan"), None)
    return jax.shard_map(
        body,
        mesh=mesh,
        in_specs=(
            rows, rows, rows, rows,
            P(None, "chan"), P(None, "chan"), P(None, "chan"), P("chan"), P("chan", None),
            P("band"), P("band"), P("band"),
        ),
        out_specs=(
            rows, rows, rows,
            P(None, "chan"), P(None, "chan"), P(None, "chan"), P("chan"), P("chan", None),
        ),
        check_vma=False,
    )
```

time: 130 us -> 96.4 us (0.74)
  Pallas kernels: 110 us -> 90.9 us
  other arithmetic: 9.43 us -> 1.2 us
  local copies, waits for them, and re-layouts: 8.31 us -> 2.7 us
    pallas_call x2 -> x3, Pallas kernels: 86.2 us -> 67.9 us  [the longest x1 39.8 us: body(): pl.pallas_call(functools.partial(reduce_kernel, low, high), out_shape=(sd...]
    convert_element_type x4 -> x0, other arithmetic: 6.2 us -> none  [the longest x3 5.33 us: body(): add = lambda a, b: (a.astype(F32) + b.astype(F32)).astype(BF)]
    transpose x3 -> x0, local copies, waits for them, and re-layouts: 3 us -> none  [the longest x1 1 us: body(): full(out_a, 0)]
    unnamed x21 -> x0, local copies, waits for them, and re-layouts: 2.57 us -> none
    reshape x5 -> x0, local copies, waits for them, and re-layouts: 1.87 us -> none  [the longest x3 1.85 us: body(): jnp.roll(v.reshape(2, rows_e), chan, axis=0).reshape(tiles, 1, tile)]
    reduce_sum x1 -> x0, other arithmetic: 1.5 us -> none  [body(): jnp.sum(bias_all[:, 0], axis=0)]
    another operation x0 -> x2, local copies, waits for them, and re-layouts: none -> 1.44 us  [body(): idx = jnp.stack([senders, receivers]).reshape(2, tiles, 1, tile)]
where the time goes in v2:
time: 96.4 us; the launch traced here: 96.1 us
  Pallas kernels  90.9 us (94%)
  local copies, waits for them, and re-layouts  2.7 us (3%)
  between operations  1.31 us (1%)
  other arithmetic  1.2 us (1%)
    pallas_call x1, Pallas kernels, body(): pl.pallas_call(functools.partial(reduce_kernel, low, high), out_shape=(sd...  39.8 us
    pallas_call x1, Pallas kernels, body(): pl.pallas_call(functools.partial(main_kernel, tiles, own_m), grid_spec=pl...  24.1 us
    pallas_call x1, Pallas kernels, body(): pl.pallas_call(functools.partial(gather_kernel, n), out_shape=(sds(grid_l...  23 us
    pallas_call x1, Pallas kernels, body(): pl.pallas_call(final_kernel, grid=(2,), in_specs=[rows_of(rows_g), rows_o...  3.97 us

profile of v2, /device:TPU:0, one launch (start us, length us, event | category | flops | bytes accessed | tf_op | source)
XLA Modules:
  0.0 96.1 jit_solution(6280735547644740260)
XLA Ops:
  1.3 0.6 pad_add_fusion.1.scal
  1.9 0.7 stack.21
  2.6 0.7 stack.22
  3.3 0.6 pad_add_fusion.idx
  3.9 23.0 %shard_map.179 = (bf16[576,512]{1,0:T(8,128)(2,1)}, bf16[1152,512]{1,0:T(8,128)(2,1)}, bf16[3,2,2,160,512]{4,3,2,1,0:T(8,128)(2,1)}) custom-call(bf16[576,512]{1,0:T(8,128)(2,1)} %grid.3, bf16[1152,512]{1,0:T(8,128)(2,1)} %edge.3, bf16[160,512]{1,0:T(8,128)(2,1)} %mesh.1, bf16[160,512]{1,0:T(8,128)(2,1)} %cot.1), custom_call_target="tpu_custom_call" | custom-call | tf_op jit(solution)/shard_map/pallas_call | solution.py:328
  26.9 24.1 %shard_map.180 = (bf16[2304,512]{1,0:T(8,128)(2,1)}, bf16[1152,512]{1,0:T(8,128)(2,1)}, bf16[960,256]{1,0:T(8,128)(2,1)}, bf16[2,16,2,16,512]{4,3,2,1,0:T(8,128)(2,1)}, f32[8,256]{1,0:T(8,128)}) custom-call(s32[3]{0:T(128)} %pad_add_fusion.1.scal, bf16[576,512]{1,0:T(8,128)(2,1)} %grid.3, bf16[576,512]{1,0:T(8,128)(2,1)} %get-tuple-element.30.grid_oth, ...), custom_call_target="tpu_custom_call" | custom-call | tf_op jit(solution)/shard_map/pallas_call | solution.py:352
  51.0 39.8 %shard_map.181 = (bf16[1152,512]{1,0:T(8,128)(2,1)}, bf16[576,512]{1,0:T(8,128)(2,1)}, bf16[160,512]{1,0:T(8,128)(2,1)}, bf16[160,512]{1,0:T(8,128)(2,1)}, bf16[...) custom-call(bf16[2304,512]{1,0:T(8,128)(2,1)} %get-tuple-element.34.grad_edge.edge_own, ...), custom_call_target="tpu_custom_call" | custom-call | tf_op jit(solution)/shard_map/pallas_call | solution.py:392
  90.9 4.0 %shard_map.182 = (bf16[576,512]{1,0:T(8,128)(2,1)}, bf16[1152,512]{1,0:T(8,128)(2,1)}, bf16[160,512]{1,0:T(8,128)(2,1)}, f32[512,256]{1,0:T(8,128)}, f32[512,256...) custom-call(bf16[1152,512]{1,0:T(8,128)(2,1)} %get-tuple-element.33.grad_grid.grid_own, ...), custom_call_target="tpu_custom_call" | custom-call | tf_op jit(solution)/shard_map/pallas_call | solution.py:419
  94.8 1.3 %slice.3 = f32[1,256]{1,0:T(1,128)} slice(f32[8,256]{1,0:T(8,128)} %get-tuple-element.50), slice={[0:1], [0:256]} | slice | bytes 2048 | tf_op jit(solution)/shard_map/slice | solution.py:443

commit v3 on v2

--- a/solution.py
+++ b/solution.py
@@ -69,12 +69,12 @@
 
 
 def main_kernel(
-    tiles, own_m, scal, grid, grid_oth, edge, edge_oth, win, wg, we, wm, wo, bias, idx,
+    tiles, own_m, used, grid, grid_oth, edge, edge_oth, win, wg, we, wm, wo, bias, sender, receiver,
     grad_edge, grad_grid, rx, gall, gbias,
     wg_t, we_t, bcol, pg, pmc, sg, sr, ge, gb,
 ):
     t = pl.program_id(0)
-    chan, band, count = scal[0], scal[1], scal[2]
+    chan, band, count = lax.axis_index("chan"), lax.axis_index("band"), used[0]
     rows, width = grid.shape
     hidden = wg.shape[1]
     window = 3 * own_m
@@ -103,9 +103,9 @@
     tile = edge.shape[0]
     x = jnp.where(t < tiles // 2, edge[...], edge_oth[...])
     place = lax.rem(t + chan * (tiles // 2), tiles)
-    from_row = idx[0, 0] - (2 * band + chan) * rows
+    from_row = sender[place] - (2 * band + chan) * rows
     from_row = jnp.where(from_row < 0, from_row + 2 * rows, from_row)
-    to_row = idx[1, 0] - (band - 1) * own_m
+    to_row = receiver[place] - (band - 1) * own_m
     owner = jnp.where(to_row >= 2 * own_m, 2 * own_m, jnp.where(to_row >= own_m, own_m, 0))
     inner = to_row - owner - chan * (own_m // 2)
     to_row = owner + jnp.where(inner < 0, inner + own_m, inner)
@@ -299,7 +299,7 @@
     gwe[...] = full(0, 1).T
     gwm[...] = full(1, 0).T
     gwo[...] = full(1, 1)
-    gbias[...] = jnp.sum(bias_out[...], axis=0)
+    gbias[...] = jnp.sum(bias_out[...], axis=0)[0]
 
 
 def body(
@@ -317,7 +317,6 @@
     edge_count,
 ):
     n = lax.axis_size("band")
-    band, chan = lax.axis_index("band"), lax.axis_index("chan")
     rows_g, width = grid_latent.shape
     rows_e = edge_latent.shape[0]
     rows_m = mesh_latent.shape[0]
@@ -337,7 +336,7 @@
         compiler_params=pltpu.CompilerParams(collective_id=0, has_side_effects=True),
     )(grid_latent, edge_latent, mesh_latent, mesh_cotangent)
 
-    tile = 384 if rows_e % 384 == 0 else rows_e
+    tile = rows_e
     tiles = 2 * rows_e // tile
     mid = tiles // 2
     padded = -(-3 * own_m // 128) * 128
@@ -346,37 +345,32 @@
         low *= 2
     high = n // low
     rows_c = hidden // n
-    scal = jnp.stack([chan, band, edge_count[0]]).astype(jnp.int32)
-    idx = jnp.stack([senders, receivers]).reshape(2, tiles, 1, tile)
-    whole = lambda *shape: pl.BlockSpec(shape, lambda t, s: (0,) * len(shape))
+    whole = lambda *shape: pl.BlockSpec(shape, lambda t: (0,) * len(shape))
     grad_edge, grad_grid, rx, gall, gbias = pl.pallas_call(
         functools.partial(main_kernel, tiles, own_m),
-        grid_spec=pltpu.PrefetchScalarGridSpec(
-            num_scalar_prefetch=1,
-            grid=(tiles,),
-            in_specs=[
-                whole(rows_g, width), whole(rows_g, width),
-                pl.BlockSpec((tile, width), lambda t, s: (jnp.minimum(t, mid - 1), 0)),
-                pl.BlockSpec((tile, width), lambda t, s: (jnp.maximum(t - mid, 0), 0)),
-                whole(3, 2, 2, rows_m, width),
-                whole(width, hidden), whole(width, hidden), whole(width, hidden),
-                whole(hidden, width), whole(1, hidden),
-                pl.BlockSpec(
-                    (2, 1, 1, tile), lambda t, s: (0, lax.rem(t + s[0] * mid, tiles), 0, 0)),
-            ],
-            out_specs=(
-                pl.BlockSpec((tile, width), lambda t, s: (t, 0)),
-                whole(2 * rows_g, width), whole(3 * own_m, hidden),
-                whole(2, n, 2, rows_c, width), whole(8, hidden),
-            ),
-            scratch_shapes=[
-                pltpu.VMEM((hidden, width), BF), pltpu.VMEM((hidden, width), BF),
-                pltpu.VMEM((hidden, 128), F32),
-                pltpu.VMEM((hidden, 2 * rows_g), BF), pltpu.VMEM((2 * hidden, padded), BF),
-                pltpu.VMEM((hidden, 2 * rows_g), F32), pltpu.VMEM((2 * hidden, padded), F32),
-                pltpu.VMEM((hidden, width), F32), pltpu.VMEM((hidden, 128), F32),
-            ],
-        ),
+        grid=(tiles,),
+        in_specs=[
+            pl.BlockSpec(memory_space=pltpu.SMEM),
+            whole(rows_g, width), whole(rows_g, width),
+            pl.BlockSpec((tile, width), lambda t: (jnp.minimum(t, mid - 1), 0)),
+            pl.BlockSpec((tile, width), lambda t: (jnp.maximum(t - mid, 0), 0)),
+            whole(3, 2, 2, rows_m, width),
+            whole(width, hidden), whole(width, hidden), whole(width, hidden),
+            whole(hidden, width), whole(1, hidden),
+            whole(tiles, 1, tile), whole(tiles, 1, tile),
+        ],
+        out_specs=(
+            pl.BlockSpec((tile, width), lambda t: (t, 0)),
+            whole(2 * rows_g, width), whole(3 * own_m, hidden),
+            whole(2, n, 2, rows_c, width), whole(8, hidden),
+        ),
+        scratch_shapes=[
+            pltpu.VMEM((hidden, width), BF), pltpu.VMEM((hidden, width), BF),
+            pltpu.VMEM((hidden, 128), F32),
+            pltpu.VMEM((hidden, 2 * rows_g), BF), pltpu.VMEM((2 * hidden, padded), BF),
+            pltpu.VMEM((hidden, 2 * rows_g), F32), pltpu.VMEM((2 * hidden, padded), F32),
+            pltpu.VMEM((hidden, width), F32), pltpu.VMEM((hidden, 128), F32),
+        ],
         out_shape=(
             sds((2 * rows_e, width), BF), sds((2 * rows_g, width), BF),
             sds((3 * own_m, hidden), BF),
@@ -384,8 +378,9 @@
         ),
         compiler_params=pltpu.CompilerParams(dimension_semantics=("arbitrary",)),
     )(
-        scal, grid_latent, grid_oth, edge_latent, edge_oth, win,
-        w_grid, w_edge, w_mesh, w_out, bias[None], idx,
+        edge_count, grid_latent, grid_oth, edge_latent, edge_oth, win,
+        w_grid, w_edge, w_mesh, w_out, bias[None],
+        senders.reshape(tiles, 1, tile), receivers.reshape(tiles, 1, tile),
     )
 
     blocks = (2, rows_c, width)
@@ -428,19 +423,19 @@
         out_specs=(
             rows_of(rows_g), rows_of(rows_e), rows_of(rows_m),
             turned_spec, turned_spec, turned_spec,
-            pl.BlockSpec((8, hidden), lambda t: (0, 0)), rows_of(hidden),
+            pl.BlockSpec((hidden,), lambda t: (0,)), rows_of(hidden),
         ),
         out_shape=(
             sds((rows_g, width), BF), sds((rows_e, width), BF), sds((rows_m, width), BF),
             sds((width, hidden), F32), sds((width, hidden), F32), sds((width, hidden), F32),
-            sds((8, hidden), F32), sds((hidden, width), F32),
+            sds((hidden,), F32), sds((hidden, width), F32),
         ),
         compiler_params=pltpu.CompilerParams(dimension_semantics=("arbitrary",)),
     )(
         grad_grid, grid_in, grad_edge, edge_in, mesh_own, mesh_in,
         out.reshape((2, n) + blocks), bias_out,
     )
-    return grad_grid, grad_edge, grad_mesh, gwg, gwm, gwe, gbias[0], gwo
+    return grad_grid, grad_edge, grad_mesh, gwg, gwm, gwe, gbias, gwo
 
 
 def solution(mesh):

time: 96.4 us -> 91.3 us (0.947)
  Pallas kernels: 90.9 us -> 87.1 us
  other arithmetic: 1.2 us -> 0 us
    pallas_call x1, Pallas kernels: 24.1 us -> 20.2 us  [body(): pl.pallas_call(functools.partial(main_kernel, tiles, own_m), grid=(tiles,...]
    reshape x0 -> x2, local copies, waits for them, and re-layouts: none -> 2.63 us  [the longest x1 1.32 us: body(): senders.reshape(tiles, 1, tile)]
    another operation x2 -> x0, local copies, waits for them, and re-layouts: 1.44 us -> none  [body(): idx = jnp.stack([senders, receivers]).reshape(2, tiles, 1, tile)]
    slice x1 -> x0, local copies, waits for them, and re-layouts: 1.26 us -> none  [body(): return (grad_grid, grad_edge, grad_mesh, gwg, gwm, gwe, gbias[0], gwo)]
    another operation x2 -> x0, other arithmetic: 1.2 us -> none  [the longest x1 0.61 us: body(): idx = jnp.stack([senders, receivers]).reshape(2, tiles, 1, tile)]
where the time goes in v3:
time: 91.3 us; the launch traced here: 91 us
  Pallas kernels  87.1 us (95%)
  local copies, waits for them, and re-layouts  2.63 us (3%)
  between operations  1.3 us (1%)
    pallas_call x1, Pallas kernels, body(): pl.pallas_call(functools.partial(reduce_kernel, low, high), out_shape=(sd...  39.9 us
    pallas_call x1, Pallas kernels, body(): pl.pallas_call(functools.partial(gather_kernel, n), out_shape=(sds(grid_l...  23 us
    pallas_call x1, Pallas kernels, body(): pl.pallas_call(functools.partial(main_kernel, tiles, own_m), grid=(tiles,...  20.2 us
    pallas_call x1, Pallas kernels, body(): pl.pallas_call(final_kernel, grid=(2,), in_specs=[rows_of(rows_g), rows_o...  3.97 us

profile of v3, /device:TPU:0, one launch (start us, length us, event | category | flops | bytes accessed | tf_op | source)
XLA Modules:
  0.0 91.0 jit_solution(18174978674188638702)
XLA Ops:
  1.3 1.3 %reshape.31.sender = s32[2,1,1152]{2,1,0:T(1,128)} reshape(s32[2304]{0:T(1024)} %param.21) | data formatting | bytes 18432 | tf_op jit(solution)/shard_map/reshape | solution.py:383
  2.6 1.3 %reshape.32.receiver = s32[2,1,1152]{2,1,0:T(1,128)} reshape(s32[2304]{0:T(1024)} %param.22) | data formatting | bytes 18432 | tf_op jit(solution)/shard_map/reshape | solution.py:383
  3.9 23.0 %shard_map.179 = (bf16[576,512]{1,0:T(8,128)(2,1)}, bf16[1152,512]{1,0:T(8,128)(2,1)}, bf16[3,2,2,160,512]{4,3,2,1,0:T(8,128)(2,1)}) custom-call(bf16[576,512]{1,0:T(8,128)(2,1)} %grid.3, bf16[1152,512]{1,0:T(8,128)(2,1)} %edge.3, bf16[160,512]{1,0:T(8,128)(2,1)} %mesh.1, bf16[160,512]{1,0:T(8,128)(2,1)} %cot.1), custom_call_target="tpu_custom_call" | custom-call | tf_op jit(solution)/shard_map/pallas_call | solution.py:327
  26.9 20.2 %shard_map.180 = (bf16[2304,512]{1,0:T(8,128)(2,1)}, bf16[1152,512]{1,0:T(8,128)(2,1)}, bf16[960,256]{1,0:T(8,128)(2,1)}, bf16[2,16,2,16,512]{4,3,2,1,0:T(8,128)(2,1)}, f32[8,256]{1,0:T(8,128)}) custom-call(s32[1]{0:T(128)S(6)} %copy.20.used, bf16[576,512]{1,0:T(8,128)(2,1)} %grid.3, bf16[576,512]{1,0:T(8,128)(2,1)} %get-tuple-element.22.grid_oth, ...), custom_call_target="tpu_custom_call" | custom-call | tf_op jit(solution)/shard_map/pallas_call | solution.py:349
  47.1 39.9 %shard_map.181 = (bf16[1152,512]{1,0:T(8,128)(2,1)}, bf16[576,512]{1,0:T(8,128)(2,1)}, bf16[160,512]{1,0:T(8,128)(2,1)}, bf16[160,512]{1,0:T(8,128)(2,1)}, bf16[...) custom-call(bf16[2304,512]{1,0:T(8,128)(2,1)} %get-tuple-element.26.grad_edge.edge_own, ...), custom_call_target="tpu_custom_call" | custom-call | tf_op jit(solution)/shard_map/pallas_call | solution.py:387
  87.0 4.0 %shard_map.182 = (bf16[576,512]{1,0:T(8,128)(2,1)}, bf16[1152,512]{1,0:T(8,128)(2,1)}, bf16[160,512]{1,0:T(8,128)(2,1)}, f32[512,256]{1,0:T(8,128)}, f32[512,256...) custom-call(bf16[1152,512]{1,0:T(8,128)(2,1)} %get-tuple-element.25.grad_grid.grid_own, ...), custom_call_target="tpu_custom_call" | custom-call | tf_op jit(solution)/shard_map/pallas_call | solution.py:414
